TPU v7x, 32 devices: a whole 2x2x4 slice. The times are simulated.
32 devices in a mesh: rows: 8 (over y, x, core), sub: 4 (over z).
Axes of the slice: x: 2, y: 2, z: 4, core: 2. Of those that a mesh axis runs over, the one named last changes fastest.
Arguments:
- u_fem: float32 [120, 524288], P(None, ('rows', 'sub')), may hold values from -600 to 600
- resid_fem: float32 [1, 524288], P(None, ('rows', 'sub')), may hold values from -60 to 60
- slot_map: int32 [32, 32], P(('rows', 'sub')), may hold values from 0 to 31, as said below
- restart: float32 [120, 40], replicated, may hold values from -0.5 to 0.5
- coeff: float32 [3, 120, 120], P(None, None, 'sub'), may hold values from -6 to 6
Outputs:
- new_basis: float32 [40, 524288], P(None, ('rows', 'sub'))
- next_vector: float32 [1, 524288], P(None, ('rows', 'sub'))
- new_coeff: float32 [3, 40, 120], replicated
Inputs may be any that keep to these rules, and one draw needn't show every extreme that they name: Each row of slot_map is a permutation of 0 to 31.
All inputs are finite; a program needn't handle non-finite values.
Results may differ from a plain program's by a relative error of at most 0.00015.
Values sent between devices are 32-bit elements; how exact they have to be, the bound alone decides.
A program may use at most 64 MiB of HBM per device.

v0:
```python
import jax
import jax.numpy as jnp
from jax import lax
from jax.sharding import PartitionSpec as P


def settle(values, source, dev_count):
    width = values.shape[0]
    block_len = values.shape[1] // dev_count
    blocks = values.reshape(width, dev_count, block_len)
    return jnp.take(blocks, source, axis=1).reshape(width, dev_count * block_len)


def local(u_fem, resid_fem, slot_map, restart, coeff):
    highest = lax.Precision.HIGHEST
    dev_count = lax.axis_size(("rows", "sub"))
    nrows_all = u_fem.shape[1] * dev_count
    source = jnp.argsort(slot_map[0])
    basis_rows, resid_row = (u_fem, resid_fem)
    gram_local = jnp.einsum("kn,jn->kj", basis_rows, basis_rows, precision=highest)
    inner_local = jnp.einsum("kn,n->k", basis_rows, resid_row[0], precision=highest)
    gram_sum = lax.psum(gram_local, ("rows", "sub"))
    chol_lower = jnp.linalg.cholesky(gram_sum / nrows_all)
    factor = lax.linalg.triangular_solve(
        chol_lower, restart, left_side=True, lower=True, transpose_a=True
    )
    new_rows = jnp.einsum("kp,kn->pn", factor, basis_rows, precision=highest)
    inner_prod = lax.psum(inner_local, ("rows", "sub"))
    half_solve = lax.linalg.triangular_solve(
        chol_lower, inner_prod[:, None], left_side=True, lower=True
    )
    proj_coef = (
        lax.linalg.triangular_solve(
            chol_lower, half_solve, left_side=True, lower=True, transpose_a=True
        )[:, 0]
        / nrows_all
    )
    remainder = resid_row - jnp.einsum("k,kn->n", proj_coef, basis_rows, precision=highest)[None, :]
    norm_sum = lax.psum(jnp.sum(remainder * remainder), ("rows", "sub"))
    next_row = remainder * lax.rsqrt(norm_sum / nrows_all + 1e-06)
    new_rows, next_row = (
        lax.all_to_all(new_rows, ("rows", "sub"), split_axis=1, concat_axis=1, tiled=True),
        lax.all_to_all(next_row, ("rows", "sub"), split_axis=1, concat_axis=1, tiled=True),
    )
    new_rows = settle(new_rows, source, dev_count)
    next_row = settle(next_row, source, dev_count)
    raised = jnp.dot(chol_lower, restart, precision=highest)
    coeff_all = lax.all_gather(coeff, "sub", axis=2, tiled=True)
    rotated = jnp.einsum("kp,ikm->ipm", raised, coeff_all, precision=highest)
    new_coeff = rotated * lax.rsqrt(jnp.mean(rotated * rotated) + 1e-06)
    return (new_rows, next_row, new_coeff)


def solution(mesh):
    in_specs = (
        P(None, ("rows", "sub")),
        P(None, ("rows", "sub")),
        P(("rows", "sub"), None),
        P(),
        P(None, None, "sub"),
    )
    out_specs = (P(None, ("rows", "sub")), P(None, ("rows", "sub")), P())
    return jax.shard_map(local, mesh=mesh, in_specs=in_specs, out_specs=out_specs, check_vma=False)
```

profile of v0, /device:TPU:0, one launch (start us, length us, event | category | flops | bytes accessed | tf_op | source)
XLA Modules:
  0.0 229.9 jit_solution(9403381852364649270)
XLA Ops:
  0.6 0.0 copy-start
  0.6 0.0 copy-start.1
  0.7 0.0 copy-start.2
  0.7 10.1 %fusion.16 = f32[120,120]{0,1:T(8,128)S(1)} fusion(f32[120,16384]{1,0:T(8,128)} %param.5), kind=kOutput, calls=%fused_computation.44 | convolution fusion | flops 2831155200 | bytes 7921920 | tf_op jit(solution)/shard_map/kn,jn->kj/dot_general | solution.py:20
  10.7 0.0 copy-done.1
  10.7 0.0 copy-done.2
  10.8 6.2 %convolution_bitcast_fusion.3 = f32[120]{0:T(128)S(1)} fusion(f32[120,16384]{1,0:T(8,128)S(1)} %copy-done.1, f32[1,16384]{1,0:T(1,128)S(1)} %copy-done.2), kind=kOutput, calls=%fused_computation.10 | convolution fusion | flops 23592960 | bytes 7930336 | tf_op jit(solution)/shard_map/kn,n->k/dot_general | solution.py:21
  16.9 42.8 %all-reduce = (f32[120,120]{0,1:T(8,128)S(1)}, f32[120]{0:T(128)S(1)}) all-reduce(f32[120,120]{0,1:T(8,128)S(1)} %fusion.16, f32[120]{0:T(128)S(1)} %convolution_bitcast_fusion.3), channel_id=1, replica_groups=mesh['rows'=8,'sub'=4] {'rows','sub'}, use_global_device_ids=true, to_apply=%region_1.2 | all-reduce | flops 14520 | bytes 116160 | tf_op jit(solution)/shard_map/psum | solution.py:22
  59.8 0.1 copy.18
  59.9 11.0 %cholesky.16 = f32[120,120]{1,0:T(8,128)S(1)} custom-call(f32[120,120]{1,0:T(8,128)S(1)} %fusion.9), custom_call_target="Cholesky" | custom-call | tf_op jit(solution)/shard_map/jit(cholesky)/cholesky | solution.py:23
  70.9 0.6 compare_reduce_fusion
  71.5 0.7 select_bitcast_fusion
  72.2 9.2 %custom-call.10 = f32[1,120,120]{1,2,0:T(8,128)S(1)} custom-call(f32[1,120,120]{2,1,0:T(8,128)S(1)} %select_bitcast_fusion), custom_call_target="InvertDiagBlocksLowerTriangular" | custom-call | tf_op jit(solution)/shard_map/triangular_solve | solution.py:24
  81.4 0.2 convolution_bitcast_fusion.2
  81.6 0.2 fusion.1
  81.8 6.7 %multiply_reduce_fusion = (f32[]{:T(128)}, f32[1,16384]{1,0:T(1,128)S(1)}) fusion(f32[1,16384]{1,0:T(1,128)S(1)} %copy-done.2, f32[120,1]{0,1:T(1,128)S(1)} %fusion.1, f32[120,16384]{1,0:T(8,128)} %param.5), kind=kOutput, calls=%fused_computation.15 | convolution fusion | flops 23642112 | bytes 7995876 | tf_op jit(solution)/shard_map/k,kn->n/dot_general | solution.py:38
  88.5 40.3 %psum.23 = f32[]{:T(128)} all-reduce(f32[]{:T(128)} %get-tuple-element.7), channel_id=1, replica_groups=mesh['rows'=8,'sub'=4] {'rows','sub'}, use_global_device_ids=true, to_apply=%region_6.7 | all-reduce | flops 1 | bytes 8 | tf_op jit(solution)/shard_map/psum | solution.py:39
  129.5 0.7 broadcast_multiply_fusion
  130.1 5.4 %all-to-all-start.1 = ((f32[1,32,512]{2,0,1:T(1,128)}), f32[1,32,512]{2,0,1:T(1,128)S(1)}, u32[]{:S(2)}, u32[]{:S(2)}) async-start(f32[1,32,512]{2,0,1:T(1,128)} %bitcast.14), calls=%async_computation.1 | async-start | bytes 131072 | tf_op jit(solution)/shard_map/all_to_all | solution.py:43
  135.5 0.0 copy-done
  135.6 0.2 fusion.7
  135.8 0.0 copy-start.4
  135.8 6.5 %fusion.17 = f32[40,16384]{1,0:T(8,128)S(1)} fusion(f32[120,40]{0,1:T(8,128)S(1)} %fusion.7, f32[120,16384]{1,0:T(8,128)} %param.5), kind=kOutput, calls=%fused_computation.45 | convolution fusion | flops 943718400 | bytes 10504960 | tf_op jit(solution)/shard_map/kp,kn->pn/dot_general | solution.py:27
  142.3 0.0 copy-start.3
  142.3 1.7 copy.36
  144.1 0.0 copy-done.4
  144.1 1.7 sort.17
  145.8 0.0 all-to-all-done.1
  145.8 5.8 %all-to-all-start = ((f32[40,32,512]{2,0,1:T(8,128)}), f32[40,32,512]{2,0,1:T(8,128)S(1)}, u32[]{:S(2)}, u32[]{:S(2)}) async-start(f32[40,32,512]{2,0,1:T(8,128)} %bitcast.69), calls=%async_computation | async-start | bytes 5242880 | tf_op jit(solution)/shard_map/all_to_all | solution.py:42
  151.6 0.1 broadcast_bitcast_fusion
  151.7 0.1 copy.28
  151.8 0.0 copy-done.3
  151.8 67.3 %all_gather.3 = f32[3,120,120]{1,0,2:T(4,128)S(1)} all-gather(f32[3,120,30]{1,0,2:T(4,128)S(1)} %copy.21), channel_id=1, replica_groups=mesh['rows'=8,'sub'=4] {'sub'}, dimensions={2}, use_global_device_ids=true | all-gather | bytes 216000 | tf_op jit(solution)/shard_map/all_gather | solution.py:48
  219.1 0.9 convolution_bitcast_fusion
  220.0 1.0 multiply_reduce_fusion.1
  221.8 0.1 broadcast_bitcast_fusion.1
  221.9 0.6 multiply_bitcast_fusion
  222.5 0.6 gather_fusion.1
  223.1 0.1 copy.29
  223.2 0.7 broadcast_select_fusion.1
  223.9 0.0 all-to-all-done
  223.9 2.2 gather_fusion
  226.2 2.1 copy.26
  228.2 1.7 broadcast_select_fusion
  (10 shorter events, 0.1 us)
Async XLA Ops:
  0.6 134.9 %copy-start = (f32[120,40]{0,1:T(8,128)S(1)}, f32[120,40]{0,1:T(8,128)}, u32[]{:S(2)}) copy-start(f32[120,40]{0,1:T(8,128)} %param.8) | copy-start | bytes 57604
  0.6 10.1 %copy-start.1 = (f32[120,16384]{1,0:T(8,128)S(1)}, f32[120,16384]{1,0:T(8,128)}, u32[]{:S(2)}) copy-start(f32[120,16384]{1,0:T(8,128)} %param.5) | copy-start | bytes 23592964
  0.7 10.1 %copy-start.2 = (f32[1,16384]{1,0:T(1,128)S(1)}, f32[1,16384]{1,0:T(1,128)}, u32[]{:S(2)}) copy-start(f32[1,16384]{1,0:T(1,128)} %param.6) | copy-start | bytes 196612
  130.1 15.6 %all-to-all-start.1 = ((f32[1,32,512]{2,0,1:T(1,128)}), f32[1,32,512]{2,0,1:T(1,128)S(1)}, u32[]{:S(2)}, u32[]{:S(2)}) async-start(f32[1,32,512]{2,0,1:T(1,128)} %bitcast.14), calls=%async_computation.1 | async-start | bytes 131072 | tf_op jit(solution)/shard_map/all_to_all | solution.py:43
  135.8 8.3 %copy-start.4 = (s32[1,32]{1,0:T(1,128)S(1)}, s32[1,32]{1,0:T(1,128)}, u32[]{:S(2)}) copy-start(s32[1,32]{1,0:T(1,128)} %param.7) | copy-start | bytes 388
  142.3 9.4 %copy-start.3 = (f32[3,120,30]{1,2,0:T(8,128)S(1)}, f32[3,120,30]{1,2,0:T(8,128)}, u32[]{:S(2)}) copy-start(f32[3,120,30]{1,2,0:T(8,128)} %param.9) | copy-start | bytes 129604
  145.8 78.2 %all-to-all-start = ((f32[40,32,512]{2,0,1:T(8,128)}), f32[40,32,512]{2,0,1:T(8,128)S(1)}, u32[]{:S(2)}, u32[]{:S(2)}) async-start(f32[40,32,512]{2,0,1:T(8,128)} %bitcast.69), calls=%async_computation | async-start | bytes 5242880 | tf_op jit(solution)/shard_map/all_to_all | solution.py:42
where the time goes:
time: 231 us; the launch traced here: 230 us
  blocking collectives  150 us (65%)
  matrix products  32 us (14%)
  other arithmetic  27 us (12%)
  starting transfers between devices  11.2 us (5%)
  local copies, waits for them, and re-layouts  7.06 us (3%)
    all_gather x1, blocking collectives, local(): coeff_all = lax.all_gather(coeff, 'sub', axis=2, tiled=True)  67.3 us
    psum x1, blocking collectives, local(): gram_sum = lax.psum(gram_local, ('rows', 'sub'))  42.8 us
    psum x1, blocking collectives, local(): norm_sum = lax.psum(jnp.sum(remainder * remainder), ('rows', 'sub'))  40.3 us
    another operation x3, other arithmetic, local(): chol_lower = jnp.linalg.cholesky(gram_sum / nrows_all)  11.6 us
    dot_general x1, matrix products, local(): jnp.einsum('kn,jn->kj', basis_rows, basis_rows, precision=highest)  10.1 us
    another operation x2, other arithmetic, local(): lax.linalg.triangular_solve(chol_lower, restart, left_side=True, lower=Tr...  9.85 us
    dot_general x1, matrix products, local(): jnp.einsum('k,kn->n', proj_coef, basis_rows, precision=highest)[None, :]  6.74 us
    dot_general x1, matrix products, local(): new_rows = jnp.einsum('kp,kn->pn', factor, basis_rows, precision=highest)  6.51 us
  transfers between devices with their start and end apart: 2, of which 0 were waited for; matrix products, arithmetic and copies ran while one was open for 6% of the time, Pallas kernels for 0%

commit v1 on v0

--- a/solution.py
+++ b/solution.py
@@ -19,7 +19,7 @@
     basis_rows, resid_row = (u_fem, resid_fem)
     gram_local = jnp.einsum("kn,jn->kj", basis_rows, basis_rows, precision=highest)
     inner_local = jnp.einsum("kn,n->k", basis_rows, resid_row[0], precision=highest)
-    gram_sum = lax.psum(gram_local, ("rows", "sub"))
+    gram_sum = lax.psum(lax.psum(gram_local, "sub"), "rows")
     chol_lower = jnp.linalg.cholesky(gram_sum / nrows_all)
     factor = lax.linalg.triangular_solve(
         chol_lower, restart, left_side=True, lower=True, transpose_a=True

time: 231 us -> 272 us (1.18)
  blocking collectives: 150 us -> 191 us
    psum x1 -> x3, blocking collectives: 42.8 us -> 82 us  [the longest x2 44.5 us: local(): gram_sum = lax.psum(lax.psum(gram_local, 'sub'), 'rows')]
  transfers between devices with their start and end apart: 2 -> 2, of which waited for: 0 -> 0; matrix products, arithmetic and copies ran while one was open for 6% -> 5% of each run, Pallas kernels for 0% -> 0%
where the time goes in v1:
time: 272 us; the launch traced here: 271 us
  blocking collectives  191 us (70%)
  matrix products  34.1 us (13%)
  other arithmetic  27 us (10%)
  starting transfers between devices  9.65 us (4%)
  local copies, waits for them, and re-layouts  6.97 us (3%)
    all_gather x1, blocking collectives, local(): coeff_all = lax.all_gather(coeff, 'sub', axis=2, tiled=True)  67.3 us
    psum x2, blocking collectives, local(): gram_sum = lax.psum(lax.psum(gram_local, 'sub'), 'rows')  44.5 us
    psum x1, blocking collectives, local(): norm_sum = lax.psum(jnp.sum(remainder * remainder), ('rows', 'sub'))  41.8 us
    psum x1, blocking collectives, local(): inner_prod = lax.psum(inner_local, ('rows', 'sub'))  37.5 us
    another operation x3, other arithmetic, local(): chol_lower = jnp.linalg.cholesky(gram_sum / nrows_all)  11.6 us
    dot_general x1, matrix products, local(): jnp.einsum('kn,jn->kj', basis_rows, basis_rows, precision=highest)  9.95 us
    another operation x2, other arithmetic, local(): lax.linalg.triangular_solve(chol_lower, restart, left_side=True, lower=Tr...  9.85 us
    dot_general x1, matrix products, local(): jnp.einsum('kn,n->k', basis_rows, resid_row[0], precision=highest)  8.42 us
  transfers between devices with their start and end apart: 2, of which 0 were waited for; matrix products, arithmetic and copies ran while one was open for 5% of the time, Pallas kernels for 0%

profile of v1, /device:TPU:0, one launch (start us, length us, event | category | flops | bytes accessed | tf_op | source)
XLA Modules:
  0.0 271.1 jit_solution(6865496560005572942)
XLA Ops:
  0.6 0.0 copy-start
  0.6 0.0 copy-start.1
  0.7 9.9 %fusion.16 = f32[120,120]{0,1:T(8,128)S(1)} fusion(f32[120,16384]{1,0:T(8,128)} %param.5), kind=kOutput, calls=%fused_computation.44 | convolution fusion | flops 2831155200 | bytes 7921920 | tf_op jit(solution)/shard_map/kn,jn->kj/dot_general | solution.py:20
  10.6 21.6 %psum.28 = f32[120,120]{0,1:T(8,128)S(1)} all-reduce(f32[120,120]{0,1:T(8,128)S(1)} %fusion.16), channel_id=1, replica_groups=mesh['rows'=8,'sub'=4] {'sub'}, use_global_device_ids=true, to_apply=%region_1.2 | all-reduce | flops 14400 | bytes 115200 | tf_op jit(solution)/shard_map/psum | solution.py:22
  32.2 22.9 %psum.29 = f32[120,120]{0,1:T(8,128)S(1)} all-reduce(f32[120,120]{0,1:T(8,128)S(1)} %psum.28), channel_id=1, replica_groups=mesh['rows'=8,'sub'=4] {'rows'}, use_global_device_ids=true, to_apply=%region_2.3 | all-reduce | flops 14400 | bytes 115200 | tf_op jit(solution)/shard_map/psum | solution.py:22
  55.2 0.1 copy.18
  55.3 11.0 %cholesky.16 = f32[120,120]{1,0:T(8,128)S(1)} custom-call(f32[120,120]{1,0:T(8,128)S(1)} %fusion.9), custom_call_target="Cholesky" | custom-call | tf_op jit(solution)/shard_map/jit(cholesky)/cholesky | solution.py:23
  66.3 0.6 compare_reduce_fusion
  66.9 0.7 select_bitcast_fusion
  67.6 9.2 %custom-call.10 = f32[1,120,120]{1,2,0:T(8,128)S(1)} custom-call(f32[1,120,120]{2,1,0:T(8,128)S(1)} %select_bitcast_fusion), custom_call_target="InvertDiagBlocksLowerTriangular" | custom-call | tf_op jit(solution)/shard_map/triangular_solve | solution.py:24
  76.8 0.0 copy-done.1
  76.8 8.4 %convolution_bitcast_fusion.3 = f32[120]{0:T(128)S(1)} fusion(f32[120,16384]{1,0:T(8,128)} %param.5, f32[1,16384]{1,0:T(1,128)S(1)} %copy-done.1), kind=kOutput, calls=%fused_computation.10 | convolution fusion | flops 23592960 | bytes 7930336 | tf_op jit(solution)/shard_map/kn,n->k/dot_general | solution.py:21
  85.2 37.5 %psum.30 = f32[120]{0:T(128)S(1)} all-reduce(f32[120]{0:T(128)S(1)} %convolution_bitcast_fusion.3), channel_id=1, replica_groups=mesh['rows'=8,'sub'=4] {'rows','sub'}, use_global_device_ids=true, to_apply=%region_5.6 | all-reduce | flops 120 | bytes 960 | tf_op jit(solution)/shard_map/psum | solution.py:28
  122.7 0.2 convolution_bitcast_fusion.2
  122.9 0.2 fusion.1
  123.1 6.7 %multiply_reduce_fusion = (f32[]{:T(128)}, f32[1,16384]{1,0:T(1,128)S(1)}) fusion(f32[1,16384]{1,0:T(1,128)S(1)} %copy-done.1, f32[120,1]{0,1:T(1,128)S(1)} %fusion.1, f32[120,16384]{1,0:T(8,128)} %param.5), kind=kOutput, calls=%fused_computation.15 | convolution fusion | flops 23642112 | bytes 7995876 | tf_op jit(solution)/shard_map/k,kn->n/dot_general | solution.py:38
  129.8 41.8 %psum.31 = f32[]{:T(128)} all-reduce(f32[]{:T(128)} %get-tuple-element.5), channel_id=1, replica_groups=mesh['rows'=8,'sub'=4] {'rows','sub'}, use_global_device_ids=true, to_apply=%region_7.8 | all-reduce | flops 1 | bytes 8 | tf_op jit(solution)/shard_map/psum | solution.py:39
  172.4 0.7 broadcast_multiply_fusion
  173.0 3.8 %all-to-all-start.1 = ((f32[1,32,512]{2,0,1:T(1,128)}), f32[1,32,512]{2,0,1:T(1,128)S(1)}, u32[]{:S(2)}, u32[]{:S(2)}) async-start(f32[1,32,512]{2,0,1:T(1,128)} %bitcast.14), calls=%async_computation.1 | async-start | bytes 131072 | tf_op jit(solution)/shard_map/all_to_all | solution.py:43
  176.9 0.0 copy-done
  176.9 0.2 fusion.7
  177.1 0.0 copy-start.3
  177.1 6.5 %fusion.17 = f32[40,16384]{1,0:T(8,128)S(1)} fusion(f32[120,40]{0,1:T(8,128)S(1)} %fusion.7, f32[120,16384]{1,0:T(8,128)} %param.5), kind=kOutput, calls=%fused_computation.45 | convolution fusion | flops 943718400 | bytes 10504960 | tf_op jit(solution)/shard_map/kp,kn->pn/dot_general | solution.py:27
  183.6 0.0 copy-start.2
  183.7 1.7 copy.36
  185.4 0.0 copy-done.3
  185.4 1.7 sort.17
  187.1 0.0 all-to-all-done.1
  187.1 5.8 %all-to-all-start = ((f32[40,32,512]{2,0,1:T(8,128)}), f32[40,32,512]{2,0,1:T(8,128)S(1)}, u32[]{:S(2)}, u32[]{:S(2)}) async-start(f32[40,32,512]{2,0,1:T(8,128)} %bitcast.69), calls=%async_computation | async-start | bytes 5242880 | tf_op jit(solution)/shard_map/all_to_all | solution.py:42
  192.9 0.1 broadcast_bitcast_fusion
  193.0 0.1 copy.28
  193.1 0.0 copy-done.2
  193.1 67.3 %all_gather.3 = f32[3,120,120]{1,0,2:T(4,128)S(1)} all-gather(f32[3,120,30]{1,0,2:T(4,128)S(1)} %copy.21), channel_id=1, replica_groups=mesh['rows'=8,'sub'=4] {'sub'}, dimensions={2}, use_global_device_ids=true | all-gather | bytes 216000 | tf_op jit(solution)/shard_map/all_gather | solution.py:48
  260.4 0.9 convolution_bitcast_fusion
  261.3 1.0 multiply_reduce_fusion.1
  263.1 0.1 broadcast_bitcast_fusion.1
  263.2 0.6 multiply_bitcast_fusion
  263.8 0.6 gather_fusion.1
  264.4 0.1 copy.29
  264.5 0.7 broadcast_select_fusion.1
  265.3 0.0 all-to-all-done
  265.3 2.2 gather_fusion
  267.5 2.0 copy.26
  269.4 1.7 broadcast_select_fusion
  (10 shorter events, 0.1 us)
Async XLA Ops:
  0.6 176.2 %copy-start = (f32[120,40]{0,1:T(8,128)S(1)}, f32[120,40]{0,1:T(8,128)}, u32[]{:S(2)}) copy-start(f32[120,40]{0,1:T(8,128)} %param.8) | copy-start | bytes 57604
  0.6 76.2 %copy-start.1 = (f32[1,16384]{1,0:T(1,128)S(1)}, f32[1,16384]{1,0:T(1,128)}, u32[]{:S(2)}) copy-start(f32[1,16384]{1,0:T(1,128)} %param.6) | copy-start | bytes 196612
  173.0 14.1 %all-to-all-start.1 = ((f32[1,32,512]{2,0,1:T(1,128)}), f32[1,32,512]{2,0,1:T(1,128)S(1)}, u32[]{:S(2)}, u32[]{:S(2)}) async-start(f32[1,32,512]{2,0,1:T(1,128)} %bitcast.14), calls=%async_computation.1 | async-start | bytes 131072 | tf_op jit(solution)/shard_map/all_to_all | solution.py:43
  177.1 8.3 %copy-start.3 = (s32[1,32]{1,0:T(1,128)S(1)}, s32[1,32]{1,0:T(1,128)}, u32[]{:S(2)}) copy-start(s32[1,32]{1,0:T(1,128)} %param.7) | copy-start | bytes 388
  183.6 9.4 %copy-start.2 = (f32[3,120,30]{1,2,0:T(8,128)S(1)}, f32[3,120,30]{1,2,0:T(8,128)}, u32[]{:S(2)}) copy-start(f32[3,120,30]{1,2,0:T(8,128)} %param.9) | copy-start | bytes 129604
  187.1 78.2 %all-to-all-start = ((f32[40,32,512]{2,0,1:T(8,128)}), f32[40,32,512]{2,0,1:T(8,128)S(1)}, u32[]{:S(2)}, u32[]{:S(2)}) async-start(f32[40,32,512]{2,0,1:T(8,128)} %bitcast.69), calls=%async_computation | async-start | bytes 5242880 | tf_op jit(solution)/shard_map/all_to_all | solution.py:42
